TPU v7x, 32 devices: a whole 2x2x4 slice. The times are simulated.
32 devices in a mesh: dp: 8 (over z, y), tensor: 4 (over x, core).
Axes of the slice: x: 2, y: 2, z: 4, core: 2. Of those that a mesh axis runs over, the one named last changes fastest.
Arguments:
- attn_out: bfloat16 [2048, 4096], P('dp', 'tensor'), may hold values from -6 to 6
- w_blocks: bfloat16 [4096, 8192], P('tensor', 'dp'), may hold values from -0.09375 to 0.09375
- w_scales: float32 [32, 8192], P('tensor', 'dp'), may hold values from 0.5 to 2
- residual: bfloat16 [2048, 8192], P('dp')
- gain: float32 [8192], P('tensor'), may hold values from 0.5 to 1.5
Outputs:
- hidden: bfloat16 [2048, 8192], P('dp', 'tensor')
- normed: bfloat16 [2048, 8192], P('dp', 'tensor')
All inputs are finite; a program needn't handle non-finite values.
Results may differ from a plain program's by a relative error of at most 0.014.
Values may be sent and summed in bfloat16 or wider, within the bound.
A program may use at most 128 MiB of HBM per device.

v0:
```python
import jax
import jax.numpy as jnp
from jax import lax
from jax.sharding import PartitionSpec as P

BLOCK = 128


def dequantize(blocks, scales):
    rows, cols = blocks.shape
    shaped = blocks.astype(jnp.float32).reshape(rows // BLOCK, BLOCK, cols)
    return (shaped * scales[:, None, :]).reshape(rows, cols).astype(jnp.bfloat16)


def on_device(attn_out, w_blocks, w_scales, residual, gain):
    everyone = lax.all_gather(attn_out, "dp", axis=0, tiled=True)
    local_cols = jnp.dot(
        everyone, dequantize(w_blocks, w_scales), preferred_element_type=jnp.float32
    )
    partial_value = lax.all_to_all(
        local_cols.astype(jnp.bfloat16), "dp", split_axis=0, concat_axis=1, tiled=True
    ).astype(local_cols.dtype)
    wide_cols = residual.shape[1]
    my_cols = gain.shape[0]
    offset = lax.axis_index("tensor") * my_cols
    total = lax.psum(partial_value.astype(jnp.bfloat16), "tensor").astype(jnp.float32)
    hidden_full = (residual.astype(jnp.float32) + total).astype(jnp.bfloat16)
    widened = hidden_full.astype(jnp.float32)
    mean_square = jnp.sum(widened * widened, axis=1, keepdims=True) / wide_cols
    mine = lax.dynamic_slice_in_dim(hidden_full, offset, my_cols, 1)
    normed = (mine.astype(jnp.float32) * gain[None, :] * lax.rsqrt(mean_square + 1e-05)).astype(
        jnp.bfloat16
    )
    return (mine, normed)


def solution(mesh):
    return jax.shard_map(
        on_device,
        mesh=mesh,
        in_specs=(
            P("dp", "tensor"),
            P("tensor", "dp"),
            P("tensor", "dp"),
            P("dp", None),
            P("tensor"),
        ),
        out_specs=(P("dp", "tensor"), P("dp", "tensor")),
        check_vma=False,
    )
```

profile of v0, /device:TPU:0, one launch (start us, length us, event | category | flops | bytes accessed | tf_op | source)
XLA Modules:
  0.0 293.9 jit_solution(12024145223568308483)
XLA Ops:
  7.2 0.0 all-gather.2.cloned.1.call-start
  7.2 0.7 all-gather.2.cloned.1.call-update
  7.9 0.0 all-reduce.2.cloned.1.call-start
  7.9 2.2 fusion
  10.1 75.5 %all-gather.2.cloned.1.call-done = bf16[2048,1024]{1,0:T(8,128)(2,1)} async-done(((bf16[256,1024]{1,0:T(8,128)(2,1)}), bf16[2048,1024]{1,0:T(8,128)(2,1)}) %all-gather.2.cloned.1.call-update) | async-done | bytes 4194320 | tf_op jit(solution)/shard_map/all_gather | solution.py:16
  85.6 7.0 %convolution_convert_fusion = bf16[1024,2048]{1,0:T(8,128)(2,1)S(1)} fusion(bf16[1024,1024]{1,0:T(8,128)(2,1)S(1)} %fusion, bf16[2048,1024]{1,0:T(8,128)(2,1)} %all-gather.2.cloned.1.call-done), kind=kOutput, calls=%fused_computation.5 | convolution fusion | flops 4297064448 | bytes 10485760 | tf_op jit(solution)/shard_map/dot_general | solution.py:17
  92.7 0.3 copy.12
  93.0 96.4 %all_to_all.19 = bf16[8,256,1024]{1,2,0:T(8,128)(2,1)} all-to-all(bf16[8,256,1024]{1,2,0:T(8,128)(2,1)S(1)} %bitcast.14), channel_id=1, replica_groups=mesh['dp'=8,'tensor'=4] {'dp'}, dimensions={0} | all-to-all | bytes 8388608 | tf_op jit(solution)/shard_map/all_to_all | solution.py:20
  189.4 6.4 %copy.9 = bf16[256,8192]{1,0:T(8,128)(2,1)} copy(bf16[256,8192]{0,1:T(8,128)(2,1)} %bitcast.15) | data formatting | bytes 8388608 | tf_op jit(solution)/shard_map/all_to_all | solution.py:20
  195.7 0.0 all-reduce.2.cloned.1.call-update
  195.8 0.0 copy-start
  195.8 84.3 %all-reduce.2.cloned.1.call-done = bf16[256,8192]{1,0:T(8,128)(2,1)} async-done(((bf16[256,8192]{1,0:T(8,128)(2,1)}), bf16[256,8192]{1,0:T(8,128)(2,1)}) %all-reduce.2.cloned.1.call-update) | async-done | bytes 4194320 | tf_op jit(solution)/shard_map/psum | solution.py:26
  280.1 5.4 %multiply_reduce_fusion = (f32[256]{0:T(256)S(1)}, bf16[256,8192]{1,0:T(8,128)(2,1)S(1)}) fusion(bf16[256,8192]{1,0:T(8,128)(2,1)} %all-reduce.2.cloned.1.call-done, bf16[256,8192]{1,0:T(8,128)(2,1)} %param.8), kind=kLoop, calls=%fused_computation | loop fusion | flops 14679808 | bytes 12583936 | tf_op jit(solution)/shard_map/reduce_sum | solution.py:29
  285.5 0.0 copy-done
  285.5 1.6 multiply_convert_fusion
  (1 shorter events, 0.0 us)
Async XLA Ops:
  7.2 78.5 %all-gather.2.cloned.1.call-start = ((), (), s32[]{:S(2)}) async-start(), calls=%async_computation.1 | async-start | bytes 4718592 | tf_op jit(solution)/shard_map/all_gather | solution.py:16
  7.9 272.2 %all-reduce.2.cloned.1.call-start = ((), (), s32[]{:S(2)}) async-start(), calls=%async_computation.2 | async-start | bytes 8388608 | tf_op jit(solution)/shard_map/psum | solution.py:26
  195.8 89.7 %copy-start = (f32[2048]{0:T(1024)S(1)}, f32[2048]{0:T(1024)}, u32[]{:S(2)}) copy-start(f32[2048]{0:T(1024)} %param.9) | copy-start | bytes 24580
Sparse Core Ops, SparseCore 0:
  10.1 75.5 all-gather.1
  195.9 84.1 all-reduce.1
where the time goes:
time: 294 us
  waiting for transfers between devices  161 us (55%)
  blocking collectives  96.4 us (33%)
  between operations  14.1 us (5%)
  other arithmetic  9.16 us (3%)
  matrix products  7.02 us (2%)
  local copies, waits for them, and re-layouts  6.65 us (2%)
    all_to_all x1, blocking collectives, on_device(): lax.all_to_all(local_cols.astype(jnp.bfloat16), 'dp', split_axis=0, conca...  96.4 us
    psum x1, waiting for transfers between devices, on_device(): lax.psum(partial_value.astype(jnp.bfloat16), 'tensor').astype(jnp.float32)  84.3 us
    all_gather x1, waiting for transfers between devices, on_device(): everyone = lax.all_gather(attn_out, 'dp', axis=0, tiled=True)  75.5 us
    dot_general x1, matrix products, on_device(): jnp.dot(everyone, dequantize(w_blocks, w_scales), preferred_element_type=...  7.02 us
    all_to_all x2, local copies, waits for them, and re-layouts, on_device(): lax.all_to_all(local_cols.astype(jnp.bfloat16), 'dp', split_axis=0, conca...  6.64 us
  transfers between devices with their start and end apart: 2, of which 2 were waited for; matrix products, arithmetic and copies ran while one was open for 1% of the time, Pallas kernels for 0%

commit v1 on v0

--- a/solution.py
+++ b/solution.py
@@ -23,7 +23,9 @@
     wide_cols = residual.shape[1]
     my_cols = gain.shape[0]
     offset = lax.axis_index("tensor") * my_cols
-    total = lax.psum(partial_value.astype(jnp.bfloat16), "tensor").astype(jnp.float32)
+    total = jnp.sum(lax.all_gather(partial_value.astype(jnp.bfloat16), "tensor"), axis=0).astype(
+        jnp.float32
+    )
     hidden_full = (residual.astype(jnp.float32) + total).astype(jnp.bfloat16)
     widened = hidden_full.astype(jnp.float32)
     mean_square = jnp.sum(widened * widened, axis=1, keepdims=True) / wide_cols

time: 294 us -> 335 us (1.14)
  local copies, waits for them, and re-layouts: 6.65 us -> 22.4 us
  waiting for transfers between devices: 161 us -> 174 us
  other arithmetic: 9.16 us -> 19.5 us
    all_gather x0 -> x1, waiting for transfers between devices: none -> 98.3 us  [on_device(): lax.all_gather(partial_value.astype(jnp.bfloat16), 'tensor')]
    psum x1 -> x0, waiting for transfers between devices: 84.3 us -> none  [on_device(): lax.psum(partial_value.astype(jnp.bfloat16), 'tensor').astype(jnp.float32)]
    unnamed x2 -> x6, local copies, waits for them, and re-layouts: 0.01 us -> 15.7 us
    reduce_sum x0 -> x1, other arithmetic: none -> 11.8 us  [on_device(): jnp.sum(lax.all_gather(partial_value.astype(jnp.bfloat16), 'tensor'), axi...]
    all_gather x0 -> x1, local copies, waits for them, and re-layouts: none -> 6.42 us  [on_device(): lax.all_gather(partial_value.astype(jnp.bfloat16), 'tensor')]
    all_to_all x2 -> x1, local copies, waits for them, and re-layouts: 6.64 us -> 0.27 us  [on_device(): lax.all_to_all(local_cols.astype(jnp.bfloat16), 'dp', split_axis=0, conca...]
  transfers between devices with their start and end apart: 2 -> 2, of which waited for: 2 -> 2; matrix products, arithmetic and copies ran while one was open for 1% -> 3% of each run, Pallas kernels for 0% -> 0%
where the time goes in v1:
time: 335 us; the launch traced here: 334 us
  waiting for transfers between devices  174 us (52%)
  blocking collectives  96.4 us (29%)
  local copies, waits for them, and re-layouts  22.4 us (7%)
  other arithmetic  19.5 us (6%)
  between operations  14.1 us (4%)
  matrix products  7.02 us (2%)
    all_gather x1, waiting for transfers between devices, on_device(): lax.all_gather(partial_value.astype(jnp.bfloat16), 'tensor')  98.3 us
    all_to_all x1, blocking collectives, on_device(): lax.all_to_all(local_cols.astype(jnp.bfloat16), 'dp', split_axis=0, conca...  96.4 us
    all_gather x1, waiting for transfers between devices, on_device(): everyone = lax.all_gather(attn_out, 'dp', axis=0, tiled=True)  75.5 us
    unnamed x6, local copies, waits for them, and re-layouts  15.7 us
    reduce_sum x1, other arithmetic, on_device(): jnp.sum(lax.all_gather(partial_value.astype(jnp.bfloat16), 'tensor'), axi...  11.8 us
    dot_general x1, matrix products, on_device(): jnp.dot(everyone, dequantize(w_blocks, w_scales), preferred_element_type=...  7.02 us
  transfers between devices with their start and end apart: 2, of which 2 were waited for; matrix products, arithmetic and copies ran while one was open for 3% of the time, Pallas kernels for 0%

profile of v1, /device:TPU:0, one launch (start us, length us, event | category | flops | bytes accessed | tf_op | source)
XLA Modules:
  0.0 334.0 jit_solution(3960304747590885534)
XLA Ops:
  7.2 0.0 all-gather.3.cloned.1.call-start
  7.2 0.7 all-gather.3.cloned.1.call-update
  7.9 0.0 all-gather.5.cloned.1.call-start
  7.9 2.2 fusion
  10.1 75.5 %all-gather.3.cloned.1.call-done = bf16[2048,1024]{1,0:T(8,128)(2,1)} async-done(((bf16[256,1024]{1,0:T(8,128)(2,1)}), bf16[2048,1024]{1,0:T(8,128)(2,1)}) %all-gather.3.cloned.1.call-update) | async-done | bytes 4194320 | tf_op jit(solution)/shard_map/all_gather | solution.py:16
  85.6 7.0 %convolution_convert_fusion = bf16[1024,2048]{1,0:T(8,128)(2,1)S(1)} fusion(bf16[1024,1024]{1,0:T(8,128)(2,1)S(1)} %fusion, bf16[2048,1024]{1,0:T(8,128)(2,1)} %all-gather.3.cloned.1.call-done), kind=kOutput, calls=%fused_computation.5 | convolution fusion | flops 4297064448 | bytes 10485760 | tf_op jit(solution)/shard_map/dot_general | solution.py:17
  92.7 0.3 copy.17
  93.0 96.4 %all_to_all.16 = bf16[8,256,1024]{1,2,0:T(8,128)(2,1)} all-to-all(bf16[8,256,1024]{1,2,0:T(8,128)(2,1)S(1)} %bitcast.14), channel_id=1, replica_groups=mesh['dp'=8,'tensor'=4] {'dp'}, dimensions={0} | all-to-all | bytes 8388608 | tf_op jit(solution)/shard_map/all_to_all | solution.py:20
  189.4 6.4 %copy.10 = bf16[1,256,8192]{2,1,0:T(8,128)(2,1)} copy(bf16[1,256,8192]{1,2,0:T(8,128)(2,1)} %bitcast.15) | data formatting | bytes 8388608 | tf_op jit(solution)/shard_map/all_gather | solution.py:26
  195.8 0.0 all-gather.5.cloned.1.call-update
  195.8 6.5 %copy.8 = bf16[256,8192]{0,1:T(8,128)(2,1)} copy(bf16[256,8192]{1,0:T(8,128)(2,1)} %param.8) | data formatting | bytes 8388608 | tf_op args[3]
  202.3 98.3 %all-gather.5.cloned.1.call-done = bf16[4,256,8192]{2,1,0:T(8,128)(2,1)} async-done(((bf16[1,256,8192]{2,1,0:T(8,128)(2,1)}), bf16[4,256,8192]{2,1,0:T(8,128)(2,1)}) %all-gather.5.cloned.1.call-update) | async-done | bytes 16777232 | tf_op jit(solution)/shard_map/all_gather | solution.py:26
  300.6 11.8 %reduce_sum.21 = bf16[256,8192]{1,0:T(8,128)(2,1)} reduce(bf16[4,256,8192]{2,1,0:T(8,128)(2,1)} %all-gather.5.cloned.1.call-done, bf16[]{:T(256)} %constant.3.clone.1), dimensions={0}, to_apply=%region_0.0 | reduce | flops 6291456 | bytes 20971522 | tf_op jit(solution)/shard_map/reduce_sum | solution.py:26
  312.3 6.4 %copy.14 = bf16[256,8192]{0,1:T(8,128)(2,1)} copy(bf16[256,8192]{1,0:T(8,128)(2,1)} %reduce_sum.21) | data formatting | bytes 8388608
  318.7 0.0 copy-start
  318.7 5.2 %multiply_reduce_fusion = (f32[256]{0:T(256)S(1)}, bf16[256,8192]{0,1:T(8,128)(2,1)S(1)}) fusion(bf16[256,8192]{0,1:T(8,128)(2,1)} %copy.14, bf16[256,8192]{0,1:T(8,128)(2,1)} %copy.8), kind=kLoop, calls=%fused_computation | loop fusion | flops 14679808 | bytes 12583936 | tf_op jit(solution)/shard_map/reduce_sum | solution.py:31
  323.9 0.0 copy-done
  323.9 0.3 multiply_convert_fusion
  324.3 1.4 copy.12
  325.7 1.4 copy.13
  (1 shorter events, 0.0 us)
Async XLA Ops:
  7.2 78.5 %all-gather.3.cloned.1.call-start = ((), (), s32[]{:S(2)}) async-start(), calls=%async_computation.1 | async-start | bytes 4718592 | tf_op jit(solution)/shard_map/all_gather | solution.py:16
  7.9 292.7 %all-gather.5.cloned.1.call-start = ((), (), s32[]{:S(2)}) async-start(), calls=%async_computation.2 | async-start | bytes 20971520 | tf_op jit(solution)/shard_map/all_gather | solution.py:26
  318.7 5.2 %copy-start = (f32[2048]{0:T(1024)S(1)}, f32[2048]{0:T(1024)}, u32[]{:S(2)}) copy-start(f32[2048]{0:T(1024)} %param.9) | copy-start | bytes 24580
Sparse Core Ops, SparseCore 0:
  10.1 75.5 all-gather.2
  195.9 104.5 all-gather.4

commit v2 on v0

--- a/solution.py
+++ b/solution.py
@@ -13,7 +13,12 @@
 
 
 def on_device(attn_out, w_blocks, w_scales, residual, gain):
-    everyone = lax.all_gather(attn_out, "dp", axis=0, tiled=True)
+    ring = [attn_out]
+    for hop in range(7):
+        ring.append(lax.ppermute(ring[-1], "dp", [(dev, (dev + 1) % 8) for dev in range(8)]))
+    everyone = jnp.roll(
+        jnp.concatenate(ring[::-1], axis=0), (lax.axis_index("dp") + 1) * ring[0].shape[0], axis=0
+    )
     local_cols = jnp.dot(
         everyone, dequantize(w_blocks, w_scales), preferred_element_type=jnp.float32
     )

time: 294 us -> 308 us (1.048)
  waiting for transfers between devices: 161 us -> 179 us
  blocking collectives: 96.4 us -> 89.9 us
    ppermute x0 -> x7, waiting for transfers between devices: none -> 95.7 us  [on_device(): lax.ppermute(ring[-1], 'dp', [(dev, (dev + 1) % 8) for dev in range(8)])]
    all_gather x1 -> x0, waiting for transfers between devices: 75.5 us -> none  [on_device(): everyone = lax.all_gather(attn_out, 'dp', axis=0, tiled=True)]
    all_to_all x1, blocking collectives: 96.4 us -> 89.9 us  [on_device(): lax.all_to_all(local_cols.astype(jnp.bfloat16), 'dp', split_axis=0, conca...]
    unnamed x2 -> x19, local copies, waits for them, and re-layouts: 0.01 us -> 4.72 us
    all_to_all x2 -> x1, local copies, waits for them, and re-layouts: 6.64 us -> 2.42 us  [on_device(): lax.all_to_all(local_cols.astype(jnp.bfloat16), 'dp', split_axis=0, conca...]
  transfers between devices with their start and end apart: 2 -> 8, of which waited for: 2 -> 8; matrix products, arithmetic and copies ran while one was open for 1% -> 1% of each run, Pallas kernels for 0% -> 0%
where the time goes in v2:
time: 308 us
  waiting for transfers between devices  179 us (58%)
  blocking collectives  89.9 us (29%)
  between operations  14.2 us (5%)
  other arithmetic  9.13 us (3%)
  local copies, waits for them, and re-layouts  7.17 us (2%)
  matrix products  4.73 us (2%)
  starting transfers between devices  3.1 us (1%)
    ppermute x7, waiting for transfers between devices, on_device(): lax.ppermute(ring[-1], 'dp', [(dev, (dev + 1) % 8) for dev in range(8)])  95.7 us
    all_to_all x1, blocking collectives, on_device(): lax.all_to_all(local_cols.astype(jnp.bfloat16), 'dp', split_axis=0, conca...  89.9 us
    psum x1, waiting for transfers between devices, on_device(): lax.psum(partial_value.astype(jnp.bfloat16), 'tensor').astype(jnp.float32)  83.7 us
  transfers between devices with their start and end apart: 8, of which 8 were waited for; matrix products, arithmetic and copies ran while one was open for 1% of the time, Pallas kernels for 0%

profile of v2, /device:TPU:0, one launch (start us, length us, event | category | flops | bytes accessed | tf_op | source)
XLA Modules:
  0.0 307.7 jit_solution(11828250418955959834)
XLA Ops:
  7.2 0.0 all-reduce.2.cloned.1.call-start
  7.2 3.0 collective-permute-start
  10.3 15.2 %collective-permute-done = bf16[256,1024]{1,0:T(8,128)(2,1)S(1)} collective-permute-done((bf16[256,1024]{1,0:T(8,128)(2,1)}, bf16[256,1024]{1,0:T(8,128)(2,1)S(1)}, u32[]{:S(2)}, u32[]{:S(2)}) %collective-permute-start) | collective-permute-done | bytes 524320 | tf_op jit(solution)/shard_map/ppermute | solution.py:18
  25.4 15.8 %collective-permute-done.1 = bf16[256,1024]{1,0:T(8,128)(2,1)S(1)} collective-permute-done((bf16[256,1024]{1,0:T(8,128)(2,1)S(1)}, bf16[256,1024]{1,0:T(8,128)(2,1)S(1)}, u32[]{:S(2)}, u32[]{:S(2)}) %collective-permute-start.1) | collective-permute-done | bytes 524320 | tf_op jit(solution)/shard_map/ppermute | solution.py:18
  41.2 0.0 collective-permute-start.2
  41.2 14.9 %collective-permute-done.2 = bf16[256,1024]{1,0:T(8,128)(2,1)S(1)} collective-permute-done((bf16[256,1024]{1,0:T(8,128)(2,1)S(1)}, bf16[256,1024]{1,0:T(8,128)(2,1)S(1)}, u32[]{:S(2)}, u32[]{:S(2)}) %collective-permute-start.2) | collective-permute-done | bytes 524320 | tf_op jit(solution)/shard_map/ppermute | solution.py:18
  56.2 0.0 collective-permute-start.3
  56.2 14.1 %collective-permute-done.3 = bf16[256,1024]{1,0:T(8,128)(2,1)S(1)} collective-permute-done((bf16[256,1024]{1,0:T(8,128)(2,1)S(1)}, bf16[256,1024]{1,0:T(8,128)(2,1)S(1)}, u32[]{:S(2)}, u32[]{:S(2)}) %collective-permute-start.3) | collective-permute-done | bytes 524320 | tf_op jit(solution)/shard_map/ppermute | solution.py:18
  70.2 13.2 %collective-permute-done.4 = bf16[256,1024]{1,0:T(8,128)(2,1)S(1)} collective-permute-done((bf16[256,1024]{1,0:T(8,128)(2,1)S(1)}, bf16[256,1024]{1,0:T(8,128)(2,1)S(1)}, u32[]{:S(2)}, u32[]{:S(2)}) %collective-permute-start.4) | collective-permute-done | bytes 524320 | tf_op jit(solution)/shard_map/ppermute | solution.py:18
  83.4 0.0 collective-permute-start.5
  83.5 12.5 %collective-permute-done.5 = bf16[256,1024]{1,0:T(8,128)(2,1)} collective-permute-done((bf16[256,1024]{1,0:T(8,128)(2,1)S(1)}, bf16[256,1024]{1,0:T(8,128)(2,1)}, u32[]{:S(2)}, u32[]{:S(2)}) %collective-permute-start.5) | collective-permute-done | bytes 524320 | tf_op jit(solution)/shard_map/ppermute | solution.py:18
  95.9 2.1 fusion
  98.1 10.0 %collective-permute-done.6 = bf16[256,1024]{1,0:T(8,128)(2,1)} collective-permute-done((bf16[256,1024]{1,0:T(8,128)(2,1)}, bf16[256,1024]{1,0:T(8,128)(2,1)}, u32[]{:S(2)}, u32[]{:S(2)}) %collective-permute-start.6) | collective-permute-done | bytes 524320 | tf_op jit(solution)/shard_map/ppermute | solution.py:18
  108.1 1.1 constant_dynamic-update-slice_fusion.15
  109.2 1.1 constant_dynamic-update-slice_fusion.14
  110.5 1.1 constant_dynamic-update-slice_fusion.7
  111.6 1.1 constant_dynamic-update-slice_fusion.6
  113.0 4.7 %fusion.3 = bf16[2048,1024]{1,0:T(8,128)(2,1)S(1)} fusion(bf16[1024,1024]{1,0:T(8,128)(2,1)S(1)} %fusion, bf16[4096,1024]{1,0:T(8,128)(2,1)S(1)} %constant_dynamic-update-slice_fusion, s32[]{:T(128)S(6)} %select_n.17), kind=kOutput, calls=%fused_computation.6 | convolution fusion | flops 4297064448 | bytes 10485764 | tf_op jit(solution)/shard_map/dot_general | solution.py:22
  117.7 89.9 %all_to_all.19 = bf16[8,256,1024]{2,1,0:T(8,128)(2,1)S(1)} all-to-all(bf16[8,256,1024]{2,1,0:T(8,128)(2,1)S(1)} %bitcast.11), channel_id=1, replica_groups=mesh['dp'=8,'tensor'=4] {'dp'}, dimensions={0} | all-to-all | bytes 8388608 | tf_op jit(solution)/shard_map/all_to_all | solution.py:25
  207.6 2.4 copy.8
  210.1 0.0 all-reduce.2.cloned.1.call-update
  210.1 83.7 %all-reduce.2.cloned.1.call-done = bf16[256,8192]{1,0:T(8,128)(2,1)} async-done(((bf16[256,8192]{1,0:T(8,128)(2,1)}), bf16[256,8192]{1,0:T(8,128)(2,1)}) %all-reduce.2.cloned.1.call-update) | async-done | bytes 4194320 | tf_op jit(solution)/shard_map/psum | solution.py:31
  293.8 5.4 %multiply_reduce_fusion = (f32[256]{0:T(256)S(1)}, bf16[256,8192]{1,0:T(8,128)(2,1)S(1)}) fusion(bf16[256,8192]{1,0:T(8,128)(2,1)} %all-reduce.2.cloned.1.call-done, bf16[256,8192]{1,0:T(8,128)(2,1)} %param.8), kind=kLoop, calls=%fused_computation | loop fusion | flops 14679808 | bytes 12583936 | tf_op jit(solution)/shard_map/reduce_sum | solution.py:34
  299.2 1.6 multiply_convert_fusion
  (20 shorter events, 0.5 us)
Async XLA Ops:
  7.2 103.3 %copy-start = (bf16[256,1024]{1,0:T(8,128)(2,1)S(1)}, bf16[256,1024]{1,0:T(8,128)(2,1)}, u32[]{:S(2)}) copy-start(bf16[256,1024]{1,0:T(8,128)(2,1)} %param.5) | copy-start | bytes 1572868
  7.2 286.6 %all-reduce.2.cloned.1.call-start = ((), (), s32[]{:S(2)}) async-start(), calls=%async_computation.1 | async-start | bytes 8388608 | tf_op jit(solution)/shard_map/psum | solution.py:31
  7.2 18.2 %collective-permute-start = (bf16[256,1024]{1,0:T(8,128)(2,1)}, bf16[256,1024]{1,0:T(8,128)(2,1)S(1)}, u32[]{:S(2)}, u32[]{:S(2)}) collective-permute-start(bf16[256,1024]{1,0:T(8,128)(2,1)} %param.5), channel_id=1, source_target_pairs={{0,4},{4,8},{8,12},{12,16},{16,20},{20,24},{24,28},{28,0},{1,5},{5... | collective-permute-start | bytes 1572872 | tf_op jit(solution)/shard_map/ppermute | solution.py:18
  25.4 15.8 %collective-permute-start.1 = (bf16[256,1024]{1,0:T(8,128)(2,1)S(1)}, bf16[256,1024]{1,0:T(8,128)(2,1)S(1)}, u32[]{:S(2)}, u32[]{:S(2)}) collective-permute-start(bf16[256,1024]{1,0:T(8,128)(2,1)S(1)} %collective-permute-done), channel_id=1, source_target_pairs={{0,4},{4,8},{8,12},{12,16},{16,20},{20,24},{24,28},{28,0},{1,5},{5... | collective-permute-start | bytes 1572872 | tf_op jit(solution)/shard_map/ppermute | solution.py:18
  41.2 14.9 %collective-permute-start.2 = (bf16[256,1024]{1,0:T(8,128)(2,1)S(1)}, bf16[256,1024]{1,0:T(8,128)(2,1)S(1)}, u32[]{:S(2)}, u32[]{:S(2)}) collective-permute-start(bf16[256,1024]{1,0:T(8,128)(2,1)S(1)} %collective-permute-done.1), channel_id=1, source_target_pairs={{0,4},{4,8},{8,12},{12,16},{16,20},{20,24},{24,28},{28,0},{1,5},{5... | collective-permute-start | bytes 1572872 | tf_op jit(solution)/shard_map/ppermute | solution.py:18
  56.2 14.1 %collective-permute-start.3 = (bf16[256,1024]{1,0:T(8,128)(2,1)S(1)}, bf16[256,1024]{1,0:T(8,128)(2,1)S(1)}, u32[]{:S(2)}, u32[]{:S(2)}) collective-permute-start(bf16[256,1024]{1,0:T(8,128)(2,1)S(1)} %collective-permute-done.2), channel_id=1, source_target_pairs={{0,4},{4,8},{8,12},{12,16},{16,20},{20,24},{24,28},{28,0},{1,5},{5... | collective-permute-start | bytes 1572872 | tf_op jit(solution)/shard_map/ppermute | solution.py:18
  70.2 13.2 %collective-permute-start.4 = (bf16[256,1024]{1,0:T(8,128)(2,1)S(1)}, bf16[256,1024]{1,0:T(8,128)(2,1)S(1)}, u32[]{:S(2)}, u32[]{:S(2)}) collective-permute-start(bf16[256,1024]{1,0:T(8,128)(2,1)S(1)} %collective-permute-done.3), channel_id=1, source_target_pairs={{0,4},{4,8},{8,12},{12,16},{16,20},{20,24},{24,28},{28,0},{1,5},{5... | collective-permute-start | bytes 1572872 | tf_op jit(solution)/shard_map/ppermute | solution.py:18
  83.4 12.5 %collective-permute-start.5 = (bf16[256,1024]{1,0:T(8,128)(2,1)S(1)}, bf16[256,1024]{1,0:T(8,128)(2,1)}, u32[]{:S(2)}, u32[]{:S(2)}) collective-permute-start(bf16[256,1024]{1,0:T(8,128)(2,1)S(1)} %collective-permute-done.4), channel_id=1, source_target_pairs={{0,4},{4,8},{8,12},{12,16},{16,20},{20,24},{24,28},{28,0},{1,5},{5... | collective-permute-start | bytes 1572872 | tf_op jit(solution)/shard_map/ppermute | solution.py:18
  95.9 12.2 %collective-permute-start.6 = (bf16[256,1024]{1,0:T(8,128)(2,1)}, bf16[256,1024]{1,0:T(8,128)(2,1)}, u32[]{:S(2)}, u32[]{:S(2)}) collective-permute-start(bf16[256,1024]{1,0:T(8,128)(2,1)} %collective-permute-done.5), channel_id=1, source_target_pairs={{0,4},{4,8},{8,12},{12,16},{16,20},{20,24},{24,28},{28,0},{1,5},{5... | collective-permute-start | bytes 1572872 | tf_op jit(solution)/shard_map/ppermute | solution.py:18
  210.1 89.1 %copy-start.1 = (f32[2048]{0:T(1024)S(1)}, f32[2048]{0:T(1024)}, u32[]{:S(2)}) copy-start(f32[2048]{0:T(1024)} %param.9) | copy-start | bytes 24580
Sparse Core Ops, SparseCore 0:
  210.2 83.5 all-reduce.1
